TPU v7x, 256 devices: a 2x2x32 block of a 4x8x32 slice. The times are simulated.
256 devices in a mesh: slides: 4 (over y, x), rows: 32 (over z), cols: 2 (over core).
Axes of the slice: x: 2, y: 2, z: 32, core: 2. Of those that a mesh axis runs over, the one named last changes fastest.
The devices are a block of a 4x8x32 slice.
Arguments:
- image: bfloat16 [4096, 512, 128], P(('slides', 'rows'), 'cols'), parts along dimension 0, may hold values from -6 to 6
- tissue: int32 [128, 16], P(('slides', 'rows'), 'cols'), parts along dimension 0, may hold values 0 or 1
- first_kernel: bfloat16 [3, 3, 128, 128], replicated, may hold values from -0.1875 to 0.1875
- first_bias: float32 [128], replicated, may hold values from -3 to 3
- second_kernel: bfloat16 [3, 3, 128, 128], replicated, may hold values from -0.1875 to 0.1875
- second_bias: float32 [128], replicated, may hold values from -3 to 3
Outputs:
- features: bfloat16 [4096, 512, 128], P(('slides', 'rows'), 'cols'), parts along dimension 0
There are 4 independent parts, one for each index of `slides`. A program takes and returns all parts, laid end to end along the dimension named above; an argument that names none is the same for every part. Nothing has to cross between parts.
All inputs are finite; a program needn't handle non-finite values. No bound on the sum of `tissue` on one device may be relied on, other than what follows from the above.
Results may differ from a plain program's by a relative error of at most 0.0043.
Values may be sent and summed in bfloat16 or wider, within the bound.
A program may use at most 128 MiB of HBM per device.

v0:
```python
import jax
import jax.numpy as jnp
from jax import lax
from jax.sharding import PartitionSpec as P

MB = 32


def with_halo(value, sides, width):
    for axis, dim in sides:
        peers, length = (lax.axis_size(axis), value.shape[dim])
        up = [(i, (i + 1) % peers) for i in range(peers - 1)]
        down = [(j, i) for i, j in up]
        last = lax.slice_in_dim(value, length - width, length, axis=dim)
        leading = lax.slice_in_dim(value, 0, width, axis=dim)
        before = lax.ppermute(last, axis, up)
        after = lax.ppermute(leading, axis, down)
        value = jnp.concatenate([before, value, after], axis=dim)
    return value


def conv_valid(padded, kernel, bias):
    rows = padded.shape[0] - 2
    cols = padded.shape[1] - 2
    chans = padded.shape[2]
    wide = jnp.concatenate(
        [padded[:, 0:cols], padded[:, 1 : cols + 1], padded[:, 2 : cols + 2]], axis=-1
    )
    total = jnp.zeros((rows * cols, kernel.shape[3]), jnp.float32)
    for offset in range(3):
        block = wide[offset : offset + rows].reshape(rows * cols, 3 * chans)
        total = total + jnp.dot(
            block,
            kernel[offset].reshape(3 * chans, kernel.shape[3]),
            preferred_element_type=jnp.float32,
        )
    return total.reshape(rows, cols, kernel.shape[3]) + bias


def shards(image, tissue, first_kernel, first_bias, second_kernel, second_bias):
    pixel_mask = jnp.repeat(jnp.repeat(tissue, MB, axis=0), MB, axis=1).astype(jnp.float32)[
        :, :, None
    ]
    padded = with_halo(image, (("rows", 0), ("cols", 1)), 1)
    hidden = (jnp.maximum(conv_valid(padded, first_kernel, first_bias), 0.0) * pixel_mask).astype(
        jnp.bfloat16
    )
    widened = with_halo(hidden, (("rows", 0), ("cols", 1)), 1)
    result = conv_valid(widened, second_kernel, second_bias)
    return (jnp.maximum(result, 0.0) * pixel_mask).astype(jnp.bfloat16)


def solution(mesh):
    in_specs = (
        P(("slides", "rows"), "cols", None),
        P(("slides", "rows"), "cols"),
        P(),
        P(),
        P(),
        P(),
    )
    out_specs = P(("slides", "rows"), "cols", None)
    return jax.shard_map(shards, mesh=mesh, in_specs=in_specs, out_specs=out_specs, check_vma=False)
```

profile of v0, /device:TPU:37, one launch (start us, length us, event | category | flops | bytes accessed | tf_op | source)
XLA Modules:
  0.0 87.2 jit_solution(4463569509391122)
XLA Ops:
  0.0 0.9 %fusion.8 = (bf16[1,256,128]{2,1,0:T(8,128)(2,1)S(1)}, bf16[1,256,128]{2,1,0:T(8,128)(2,1)S(1)}) fusion(bf16[32,256,128]{2,1,0:T(8,128)(2,1)} %param.6), kind=kLoop, calls=%fused_computation.29 | loop fusion | bytes 262144 | tf_op jit(solution)/shard_map/slice | solution.py:15
  0.9 4.6 %collective-permute-start = (bf16[1,256,128]{2,1,0:T(8,128)(2,1)S(1)}, bf16[1,256,128]{2,1,0:T(8,128)(2,1)S(1)}, u32[]{:S(2)}, u32[]{:S(2)}) collective-permute-start(bf16[1,256,128]{2,1,0:T(8,128)(2,1)S(1)} %get-tuple-element.18), channel_id=1, source_target_pairs={{0,2},{2,4},{4,6},{6,8},{8,10},{10,12},{12,14},{14,16},{16,18},{18... | collective-permute-start | bytes 196616 | tf_op jit(solution)/shard_map/ppermute | solution.py:16
  5.5 1.3 %collective-permute-start.1 = (bf16[1,256,128]{2,1,0:T(8,128)(2,1)S(1)}, bf16[1,256,128]{2,1,0:T(8,128)(2,1)S(1)}, u32[]{:S(2)}, u32[]{:S(2)}) collective-permute-start(bf16[1,256,128]{2,1,0:T(8,128)(2,1)S(1)} %get-tuple-element.17), channel_id=1, source_target_pairs={{2,0},{4,2},{6,4},{8,6},{10,8},{12,10},{14,12},{16,14},{18,16},{20... | collective-permute-start | bytes 196616 | tf_op jit(solution)/shard_map/ppermute | solution.py:17
  6.8 1.0 %fusion.10 = (bf16[1,3,128,128]{3,2,1,0:T(8,128)(2,1)S(1)}, bf16[1,3,128,128]{3,2,1,0:T(8,128)(2,1)S(1)}, bf16[1,3,128,128]{3,2,1,0:T(8,128)(2,1)S(1)}) fusion(bf16[3,3,128,128]{3,2,1,0:T(8,128)(2,1)} %param.8), kind=kLoop, calls=%fused_computation.31 | loop fusion | bytes 589824 | tf_op jit(solution)/shard_map/slice | solution.py:34
  7.8 1.9 %constant_dynamic-update-slice_fusion.1 = bf16[34,256,128]{2,1,0:T(8,128)(2,1)S(1)} fusion(bf16[34,256,128]{2,1,0:T(8,128)(2,1)S(1)} %constant_dynamic-update-slice_fusion.2, bf16[32,256,128]{2,1,0:T(8,128)(2,1)} %param.6), kind=kLoop, calls=%fused_computation.22 | loop fusion | bytes 4194304
  9.8 1.1 %collective-permute-done.1 = bf16[1,256,128]{2,1,0:T(8,128)(2,1)S(1)} collective-permute-done((bf16[1,256,128]{2,1,0:T(8,128)(2,1)S(1)}, bf16[1,256,128]{2,1,0:T(8,128)(2,1)S(1)}, u32[]{:S(2)}, u32[]{:S(2)}) %collective-permute-start.1) | collective-permute-done | bytes 65568 | tf_op jit(solution)/shard_map/ppermute | solution.py:17
  11.0 1.3 %collective-permute-start.2 = (bf16[34,1,128]{2,1,0:T(2,128)(2,1)S(1)}, bf16[34,1,128]{2,1,0:T(2,128)(2,1)S(1)}, u32[]{:S(2)}, u32[]{:S(2)}) collective-permute-start(bf16[34,1,128]{2,1,0:T(2,128)(2,1)S(1)} %get-tuple-element.13), channel_id=1, source_target_pairs={{0,1},{2,3},{4,5},{6,7},{8,9},{10,11},{12,13},{14,15},{16,17},{18,... | collective-permute-start | bytes 26120 | tf_op jit(solution)/shard_map/ppermute | solution.py:16
  12.3 19.8 %collective-permute-start.3 = (bf16[34,1,128]{2,1,0:T(2,128)(2,1)S(1)}, bf16[34,1,128]{2,1,0:T(2,128)(2,1)S(1)}, u32[]{:S(2)}, u32[]{:S(2)}) collective-permute-start(bf16[34,1,128]{2,1,0:T(2,128)(2,1)S(1)} %get-tuple-element.14), channel_id=1, source_target_pairs={{1,0},{3,2},{5,4},{7,6},{9,8},{11,10},{13,12},{15,14},{17,16},{19,... | collective-permute-start | bytes 26120 | tf_op jit(solution)/shard_map/ppermute | solution.py:17
  32.9 4.5 %fusion.2 = bf16[34,256,384]{2,1,0:T(8,128)(2,1)S(1)} fusion(bf16[34,1,128]{2,1,0:T(2,128)(2,1)S(1)} %collective-permute-done.3, bf16[34,256,128]{2,1,0:T(8,128)(2,1)S(1)} %constant_dynamic-update-slice_fusion, bf16[34,1,128]{2,1,0:T(2,128)(2,1)S(1)} %collective-permute-done.2), kind=kLoop, calls=%fused_computation.13 | loop fusion | flops 33423360 | bytes 8930304 | tf_op jit(solution)/shard_map/concatenate | solution.py:26
  37.4 6.3 %fusion.5 = (bf16[32,256,384]{2,1,0:T(8,128)(2,1)S(1)}, bf16[32,256,384]{2,1,0:T(8,128)(2,1)S(1)}, bf16[32,256,384]{2,1,0:T(8,128)(2,1)S(1)}) fusion(bf16[34,256,384]{2,1,0:T(8,128)(2,1)S(1)} %fusion.2), kind=kLoop, calls=%fused_computation.26 | loop fusion | bytes 37748736 | tf_op jit(solution)/shard_map/slice | solution.py:31
  43.7 1.8 %fusion.11 = f32[8192,128]{1,0:T(8,128)S(1)} fusion(bf16[8192,384]{1,0:T(8,128)(2,1)S(1)} %bitcast.32, bf16[384,128]{1,0:T(8,128)(2,1)S(1)} %bitcast.38), kind=kOutput, calls=%fused_computation.32 | convolution fusion | flops 805306368 | bytes 10584064 | tf_op jit(solution)/shard_map/dot_general | solution.py:32
  45.5 1.8 %convolution_add_fusion.3 = f32[8192,128]{1,0:T(8,128)S(1)} fusion(f32[8192,128]{1,0:T(8,128)S(1)} %fusion.11, bf16[8192,384]{1,0:T(8,128)(2,1)S(1)} %bitcast.30, bf16[384,128]{1,0:T(8,128)(2,1)S(1)} %bitcast.37), kind=kOutput, calls=%fused_computation.3 | convolution fusion | flops 806354944 | bytes 14778368 | tf_op jit(solution)/shard_map/dot_general | solution.py:32
  47.3 1.8 %convolution_add_fusion.2 = f32[8192,128]{1,0:T(8,128)S(1)} fusion(f32[8192,128]{1,0:T(8,128)S(1)} %convolution_add_fusion.3, bf16[8192,384]{1,0:T(8,128)(2,1)S(1)} %bitcast.28, bf16[384,128]{1,0:T(8,128)(2,1)S(1)} %bitcast.36), kind=kOutput, calls=%fused_computation.2 | convolution fusion | flops 806354944 | bytes 14778368 | tf_op jit(solution)/shard_map/dot_general | solution.py:32
  49.9 2.4 %collective-permute-start.4 = (bf16[1,256,128]{2,1,0:T(8,128)(2,1)S(1)}, bf16[1,256,128]{2,1,0:T(8,128)(2,1)S(1)}, u32[]{:S(2)}, u32[]{:S(2)}) collective-permute-start(bf16[1,256,128]{2,1,0:T(8,128)(2,1)S(1)} %get-tuple-element.15), channel_id=1, source_target_pairs={{0,2},{2,4},{4,6},{6,8},{8,10},{10,12},{12,14},{14,16},{16,18},{18... | collective-permute-start | bytes 196616 | tf_op jit(solution)/shard_map/ppermute | solution.py:16
  52.4 1.3 %collective-permute-start.5 = (bf16[1,256,128]{2,1,0:T(8,128)(2,1)S(1)}, bf16[1,256,128]{2,1,0:T(8,128)(2,1)S(1)}, u32[]{:S(2)}, u32[]{:S(2)}) collective-permute-start(bf16[1,256,128]{2,1,0:T(8,128)(2,1)S(1)} %get-tuple-element.16), channel_id=1, source_target_pairs={{2,0},{4,2},{6,4},{8,6},{10,8},{12,10},{14,12},{16,14},{18,16},{20... | collective-permute-start | bytes 196616 | tf_op jit(solution)/shard_map/ppermute | solution.py:17
  53.7 3.7 %collective-permute-done.5 = bf16[1,256,128]{2,1,0:T(8,128)(2,1)S(1)} collective-permute-done((bf16[1,256,128]{2,1,0:T(8,128)(2,1)S(1)}, bf16[1,256,128]{2,1,0:T(8,128)(2,1)S(1)}, u32[]{:S(2)}, u32[]{:S(2)}) %collective-permute-start.5) | collective-permute-done | bytes 65568 | tf_op jit(solution)/shard_map/ppermute | solution.py:17
  57.4 1.3 %collective-permute-start.6 = (bf16[34,1,128]{2,1,0:T(2,128)(2,1)S(1)}, bf16[34,1,128]{2,1,0:T(2,128)(2,1)S(1)}, u32[]{:S(2)}, u32[]{:S(2)}) collective-permute-start(bf16[34,1,128]{2,1,0:T(2,128)(2,1)S(1)} %get-tuple-element.11), channel_id=1, source_target_pairs={{0,1},{2,3},{4,5},{6,7},{8,9},{10,11},{12,13},{14,15},{16,17},{18,... | collective-permute-start | bytes 26120 | tf_op jit(solution)/shard_map/ppermute | solution.py:16
  58.8 3.9 %collective-permute-start.7 = (bf16[34,1,128]{2,1,0:T(2,128)(2,1)S(1)}, bf16[34,1,128]{2,1,0:T(2,128)(2,1)S(1)}, u32[]{:S(2)}, u32[]{:S(2)}) collective-permute-start(bf16[34,1,128]{2,1,0:T(2,128)(2,1)S(1)} %get-tuple-element.12), channel_id=1, source_target_pairs={{1,0},{3,2},{5,4},{7,6},{9,8},{11,10},{13,12},{15,14},{17,16},{19,... | collective-permute-start | bytes 26120 | tf_op jit(solution)/shard_map/ppermute | solution.py:17
  63.3 10.2 %fusion = bf16[34,256,384]{2,1,0:T(8,128)(2,1)S(1)} fusion(bf16[34,1,128]{2,1,0:T(2,128)(2,1)S(1)} %collective-permute-done.7, bf16[1,256,128]{2,1,0:T(8,128)(2,1)S(1)} %collective-permute-done.5, bf16[32,256,128]{2,1,0:T(8,128)(2,1)S(1)} %multiply_convert_fusion.1, bf16[1,256,128]{2,1,0:T(8,128)(2,1)S(1)} %collective-permute-done.4, ...), kind=kLoop, calls=%fused_computation.5 | loop fusion | flops 73531392 | bytes 8930304 | tf_op jit(solution)/shard_map/concatenate | solution.py:26
  73.4 6.3 %fusion.4 = (bf16[32,256,384]{2,1,0:T(8,128)(2,1)S(1)}, bf16[32,256,384]{2,1,0:T(8,128)(2,1)S(1)}, bf16[32,256,384]{2,1,0:T(8,128)(2,1)S(1)}) fusion(bf16[34,256,384]{2,1,0:T(8,128)(2,1)S(1)} %fusion), kind=kLoop, calls=%fused_computation.25 | loop fusion | bytes 37748736 | tf_op jit(solution)/shard_map/slice | solution.py:31
  79.7 1.8 %fusion.12 = f32[8192,128]{1,0:T(8,128)S(1)} fusion(bf16[8192,384]{1,0:T(8,128)(2,1)S(1)} %bitcast.33, bf16[384,128]{1,0:T(8,128)(2,1)S(1)} %bitcast.41), kind=kOutput, calls=%fused_computation.33 | convolution fusion | flops 805306368 | bytes 10584064 | tf_op jit(solution)/shard_map/dot_general | solution.py:32
  81.5 1.8 %convolution_add_fusion.1 = f32[8192,128]{1,0:T(8,128)S(1)} fusion(f32[8192,128]{1,0:T(8,128)S(1)} %fusion.12, bf16[8192,384]{1,0:T(8,128)(2,1)S(1)} %bitcast.31, bf16[384,128]{1,0:T(8,128)(2,1)S(1)} %bitcast.40), kind=kOutput, calls=%fused_computation.1 | convolution fusion | flops 806354944 | bytes 14778368 | tf_op jit(solution)/shard_map/dot_general | solution.py:32
  83.3 1.8 %convolution_add_fusion = f32[8192,128]{1,0:T(8,128)S(1)} fusion(f32[8192,128]{1,0:T(8,128)S(1)} %convolution_add_fusion.1, bf16[8192,384]{1,0:T(8,128)(2,1)S(1)} %bitcast.29, bf16[384,128]{1,0:T(8,128)(2,1)S(1)} %bitcast.39), kind=kOutput, calls=%fused_computation | convolution fusion | flops 806354944 | bytes 14778368 | tf_op jit(solution)/shard_map/dot_general | solution.py:32
  85.1 2.0 %multiply_convert_fusion = bf16[32,256,128]{2,1,0:T(8,128)(2,1)} fusion(f32[32,256,128]{2,1,0:T(8,128)S(1)} %bitcast.34, f32[128]{0:T(128)S(1)} %copy-done.2, f32[256]{0:T(256)S(1)} %convert_element_type.20), kind=kLoop, calls=%fused_computation.16 | loop fusion | flops 4194304 | bytes 6292992 | tf_op jit(solution)/shard_map/convert_element_type | solution.py:50
  (22 shorter events, 2.3 us)
Async XLA Ops:
  0.9 6.9 %collective-permute-start = (bf16[1,256,128]{2,1,0:T(8,128)(2,1)S(1)}, bf16[1,256,128]{2,1,0:T(8,128)(2,1)S(1)}, u32[]{:S(2)}, u32[]{:S(2)}) collective-permute-start(bf16[1,256,128]{2,1,0:T(8,128)(2,1)S(1)} %get-tuple-element.18), channel_id=1, source_target_pairs={{0,2},{2,4},{4,6},{6,8},{8,10},{10,12},{12,14},{14,16},{16,18},{18... | collective-permute-start | bytes 196616 | tf_op jit(solution)/shard_map/ppermute | solution.py:16
  5.5 5.4 %collective-permute-start.1 = (bf16[1,256,128]{2,1,0:T(8,128)(2,1)S(1)}, bf16[1,256,128]{2,1,0:T(8,128)(2,1)S(1)}, u32[]{:S(2)}, u32[]{:S(2)}) collective-permute-start(bf16[1,256,128]{2,1,0:T(8,128)(2,1)S(1)} %get-tuple-element.17), channel_id=1, source_target_pairs={{2,0},{4,2},{6,4},{8,6},{10,8},{12,10},{14,12},{16,14},{18,16},{20... | collective-permute-start | bytes 196616 | tf_op jit(solution)/shard_map/ppermute | solution.py:17
  11.0 22.0 %collective-permute-start.2 = (bf16[34,1,128]{2,1,0:T(2,128)(2,1)S(1)}, bf16[34,1,128]{2,1,0:T(2,128)(2,1)S(1)}, u32[]{:S(2)}, u32[]{:S(2)}) collective-permute-start(bf16[34,1,128]{2,1,0:T(2,128)(2,1)S(1)} %get-tuple-element.13), channel_id=1, source_target_pairs={{0,1},{2,3},{4,5},{6,7},{8,9},{10,11},{12,13},{14,15},{16,17},{18,... | collective-permute-start | bytes 26120 | tf_op jit(solution)/shard_map/ppermute | solution.py:16
  12.3 20.7 %collective-permute-start.3 = (bf16[34,1,128]{2,1,0:T(2,128)(2,1)S(1)}, bf16[34,1,128]{2,1,0:T(2,128)(2,1)S(1)}, u32[]{:S(2)}, u32[]{:S(2)}) collective-permute-start(bf16[34,1,128]{2,1,0:T(2,128)(2,1)S(1)} %get-tuple-element.14), channel_id=1, source_target_pairs={{1,0},{3,2},{5,4},{7,6},{9,8},{11,10},{13,12},{15,14},{17,16},{19,... | collective-permute-start | bytes 26120 | tf_op jit(solution)/shard_map/ppermute | solution.py:17
  47.3 1.8 %copy-start.1 = (f32[128]{0:T(128)S(1)}, f32[128]{0:T(128)}, u32[]{:S(2)}) copy-start(f32[128]{0:T(128)} %param.9) | copy-start | bytes 1540
  49.1 13.5 %copy-start = (bf16[3,3,128,128]{3,2,1,0:T(8,128)(2,1)S(1)}, bf16[3,3,128,128]{3,2,1,0:T(8,128)(2,1)}, u32[]{:S(2)}) copy-start(bf16[3,3,128,128]{3,2,1,0:T(8,128)(2,1)} %param.10) | copy-start | bytes 884740
  49.9 3.8 %collective-permute-start.4 = (bf16[1,256,128]{2,1,0:T(8,128)(2,1)S(1)}, bf16[1,256,128]{2,1,0:T(8,128)(2,1)S(1)}, u32[]{:S(2)}, u32[]{:S(2)}) collective-permute-start(bf16[1,256,128]{2,1,0:T(8,128)(2,1)S(1)} %get-tuple-element.15), channel_id=1, source_target_pairs={{0,2},{2,4},{4,6},{6,8},{8,10},{10,12},{12,14},{14,16},{16,18},{18... | collective-permute-start | bytes 196616 | tf_op jit(solution)/shard_map/ppermute | solution.py:16
  52.4 5.0 %collective-permute-start.5 = (bf16[1,256,128]{2,1,0:T(8,128)(2,1)S(1)}, bf16[1,256,128]{2,1,0:T(8,128)(2,1)S(1)}, u32[]{:S(2)}, u32[]{:S(2)}) collective-permute-start(bf16[1,256,128]{2,1,0:T(8,128)(2,1)S(1)} %get-tuple-element.16), channel_id=1, source_target_pairs={{2,0},{4,2},{6,4},{8,6},{10,8},{12,10},{14,12},{16,14},{18,16},{20... | collective-permute-start | bytes 196616 | tf_op jit(solution)/shard_map/ppermute | solution.py:17
  57.4 5.2 %collective-permute-start.6 = (bf16[34,1,128]{2,1,0:T(2,128)(2,1)S(1)}, bf16[34,1,128]{2,1,0:T(2,128)(2,1)S(1)}, u32[]{:S(2)}, u32[]{:S(2)}) collective-permute-start(bf16[34,1,128]{2,1,0:T(2,128)(2,1)S(1)} %get-tuple-element.11), channel_id=1, source_target_pairs={{0,1},{2,3},{4,5},{6,7},{8,9},{10,11},{12,13},{14,15},{16,17},{18,... | collective-permute-start | bytes 26120 | tf_op jit(solution)/shard_map/ppermute | solution.py:16
  58.8 4.5 %collective-permute-start.7 = (bf16[34,1,128]{2,1,0:T(2,128)(2,1)S(1)}, bf16[34,1,128]{2,1,0:T(2,128)(2,1)S(1)}, u32[]{:S(2)}, u32[]{:S(2)}) collective-permute-start(bf16[34,1,128]{2,1,0:T(2,128)(2,1)S(1)} %get-tuple-element.12), channel_id=1, source_target_pairs={{1,0},{3,2},{5,4},{7,6},{9,8},{11,10},{13,12},{15,14},{17,16},{19,... | collective-permute-start | bytes 26120 | tf_op jit(solution)/shard_map/ppermute | solution.py:17
  83.3 1.8 %copy-start.2 = (f32[128]{0:T(128)S(1)}, f32[128]{0:T(128)}, u32[]{:S(2)}) copy-start(f32[128]{0:T(128)} %param.11) | copy-start | bytes 1540
where the time goes:
time: 87.5 us; the launch traced here: 87.2 us
  starting transfers between devices  36 us (41%)
  other arithmetic  18.1 us (21%)
  local copies, waits for them, and re-layouts  16.6 us (19%)
  matrix products  10.8 us (12%)
  waiting for transfers between devices  5.43 us (6%)
    ppermute x4, starting transfers between devices, with_halo(): after = lax.ppermute(leading, axis, down)  26.3 us
    concatenate x2, other arithmetic, conv_valid(): jnp.concatenate([padded[:, 0:cols], padded[:, 1:cols + 1], padded[:, 2:co...  14.7 us
    slice x2, local copies, waits for them, and re-layouts, conv_valid(): block = wide[offset:offset + rows].reshape(rows * cols, 3 * chans)  12.5 us
    dot_general x6, matrix products, conv_valid(): jnp.dot(block, kernel[offset].reshape(3 * chans, kernel.shape[3]), prefer...  10.8 us
    ppermute x4, starting transfers between devices, with_halo(): before = lax.ppermute(last, axis, up)  9.65 us
    ppermute x4, waiting for transfers between devices, with_halo(): after = lax.ppermute(leading, axis, down)  5.42 us
    convert_element_type x1, other arithmetic, shards(): return (jnp.maximum(result, 0.0) * pixel_mask).astype(jnp.bfloat16)  2.03 us
    unnamed x8, local copies, waits for them, and re-layouts  1.98 us
  transfers between devices with their start and end apart: 8, of which 3 were waited for; matrix products, arithmetic and copies ran while one was open for 4% of the time, Pallas kernels for 0%

commit v1 on v0

v1 whole, which is shorter than its diff:
```python
import functools

import jax
import jax.numpy as jnp
from jax import lax
from jax.experimental import pallas as pl
from jax.experimental.pallas import tpu as pltpu
from jax.sharding import PartitionSpec as P

MESH = pl.DeviceIdType.MESH
MB = 32
BF = jnp.bfloat16
F32 = jnp.float32
UP, DOWN, SIDE, DUP, DDN = range(5)


def kernel(
    image, tissue, k1, b1, k2, b2, out,
    xr, xm, xp, pb, col, sm, s0, sp, h0, hm, hp, hs, w1, w2, bs, ts, mk, mks, fb, sf, ob,
    in_sem, out_sem, send_x, recv_x, send_t, recv_t,
):
    R, W, C = image.shape
    H = W // MB
    n = lax.axis_size("rows")
    sl, i, c = lax.axis_index("slides"), lax.axis_index("rows"), lax.axis_index("cols")
    has_up, has_down = i > 0, i < n - 1
    side0 = jnp.where(c == 0, 1.0, 0.0).astype(F32)
    side1 = 1.0 - side0
    edge = pl.multiple_of((W - 16) * (1 - c), 16)

    def load(src, dst, k):
        cp = pltpu.make_async_copy(src, dst, in_sem.at[k])
        cp.start()
        return cp

    l_top = load(image.at[0:2], xr.at[2:4], 0)
    l_bot = load(image.at[R - 2 : R], xr.at[R : R + 2], 1)
    l_col = load(image.at[:, pl.ds(edge, 16), :], col, 2)
    l_tis = load(tissue, ts.at[0], 3)
    l_w1 = [load(k1, w1.at[j * 3 * C : j * 3 * C + 9 * C, j * C : (j + 1) * C], 4 + j) for j in range(2)]
    l_img = load(image.at[2 : R - 2], xr.at[4:R], 6)
    l_b1 = load(b1, bs.at[0], 7)
    l_w2 = [load(k2, w2.at[j * 3 * C : j * 3 * C + 9 * C, j * C : (j + 1) * C], 8 + j) for j in range(2)]
    l_b2 = load(b2, bs.at[1], 10)

    up, down = (sl, i - 1, c), (sl, i + 1, c)
    dup, ddn, side = (sl, i - 1, 1 - c), (sl, i + 1, 1 - c), (sl, i, 1 - c)
    barrier = pltpu.get_barrier_semaphore()
    pl.semaphore_signal(barrier, inc=1, device_id=side, device_id_type=MESH)

    @pl.when(has_up)
    def _():
        pl.semaphore_signal(barrier, inc=1, device_id=up, device_id_type=MESH)
        pl.semaphore_signal(barrier, inc=1, device_id=dup, device_id_type=MESH)

    @pl.when(has_down)
    def _():
        pl.semaphore_signal(barrier, inc=1, device_id=down, device_id_type=MESH)
        pl.semaphore_signal(barrier, inc=1, device_id=ddn, device_id_type=MESH)

    for w in (w1, w2):
        w[9 * C : 12 * C, 0:C] = jnp.zeros((3 * C, C), BF)
        w[0 : 3 * C, C : 2 * C] = jnp.zeros((3 * C, C), BF)

    @pl.when(jnp.logical_not(has_up))
    def _():
        xr[0:2] = jnp.zeros((2, W, C), BF)
        pb[0:2] = jnp.zeros((2, 16, C), BF)
        ts[2] = jnp.zeros((1, H), jnp.int32)
        ts[4] = jnp.zeros((1, H), jnp.int32)

    @pl.when(jnp.logical_not(has_down))
    def _():
        xr[R + 2 : R + 4] = jnp.zeros((2, W, C), BF)
        pb[R + 2 : R + 4] = jnp.zeros((2, 16, C), BF)
        ts[3] = jnp.zeros((1, H), jnp.int32)
        ts[5] = jnp.zeros((1, H), jnp.int32)

    pl.semaphore_wait(barrier, 1 + 2 * has_up.astype(jnp.int32) + 2 * has_down.astype(jnp.int32))

    def remote(src, dst, sends, recvs, k, dev):
        return pltpu.make_async_remote_copy(
            src_ref=src, dst_ref=dst, send_sem=sends.at[k], recv_sem=recvs.at[k],
            device_id=dev, device_id_type=MESH,
        )

    r_up = remote(xr.at[2:4], xr.at[R + 2 : R + 4], send_x, recv_x, UP, up)
    r_down = remote(xr.at[R : R + 2], xr.at[0:2], send_x, recv_x, DOWN, down)
    r_side = remote(col, pb.at[2 : R + 2], send_x, recv_x, SIDE, side)
    r_dup = remote(col.at[0:2], pb.at[R + 2 : R + 4], send_x, recv_x, DUP, dup)
    r_ddn = remote(col.at[R - 2 : R], pb.at[0:2], send_x, recv_x, DDN, ddn)
    t_side = remote(ts.at[0], ts.at[1], send_t, recv_t, SIDE, side)
    t_down = remote(ts.at[0], ts.at[2], send_t, recv_t, DOWN, down)
    t_up = remote(ts.at[0], ts.at[3], send_t, recv_t, UP, up)
    t_ddn = remote(ts.at[0], ts.at[4], send_t, recv_t, DDN, ddn)
    t_dup = remote(ts.at[0], ts.at[5], send_t, recv_t, DUP, dup)

    l_top.wait()
    l_bot.wait()
    l_col.wait()
    l_tis.wait()
    r_side.start()
    t_side.start()

    @pl.when(has_up)
    def _():
        r_up.start()
        r_dup.start()
        t_up.start()
        t_dup.start()

    @pl.when(has_down)
    def _():
        r_down.start()
        r_ddn.start()
        t_down.start()
        t_ddn.start()

    def block_mask(slot, store):
        t = ts[slot].astype(F32)
        for j in range(H):
            mk[store, j] = jnp.broadcast_to(t[:, j : j + 1], (8, C))

    def strip_mask(slot, store):
        t = ts[slot].astype(F32)
        m = t[:, 0:1] * side0 + t[:, H - 1 : H] * side1
        mks[store] = jnp.broadcast_to(m, (8, C))

    block_mask(0, 0)
    for cp in l_w1:
        cp.wait()
    l_b1.wait()
    l_b2.wait()
    for cp in l_w2:
        cp.wait()
    l_img.wait()
    r_side.wait_recv()
    t_side.wait_recv()
    strip_mask(1, 0)

    counter = [0]

    def spread(value, left8, right8, r, center, minus, plus):
        f = fb.at[counter[0] % 4]
        counter[0] += 1
        f[0:8] = left8
        f[8 : W + 8] = value
        f[W + 8 : W + 16] = right8
        minus[r] = f[7 : W + 7].astype(BF)
        plus[r] = f[9 : W + 9].astype(BF)
        if center is not None:
            center[r] = value.astype(BF)

    def image_row(r):
        part = pb[r].astype(F32)
        own = xr[r, pl.ds(edge, 16), :].astype(F32)
        sf[r, pl.ds(pl.multiple_of(16 * c, 16), 16), :] = own
        sf[r, pl.ds(pl.multiple_of(16 * (1 - c), 16), 16), :] = part
        sm[r] = sf[r, 7:23].astype(BF)
        s0[r] = sf[r, 8:24].astype(BF)
        sp[r] = sf[r, 9:25].astype(BF)
        spread(xr[r].astype(F32), part[8:16] * side1, part[0:8] * side0, r, None, xm, xp)

    def lhs(p, refs):
        return jnp.concatenate([ref[2 * p + k] for k in range(4) for ref in refs], axis=1)

    bias1 = jnp.broadcast_to(bs[0], (8, C))
    bias2 = jnp.broadcast_to(bs[1], (8, C))

    def finish(acc, bias, store):
        z = jnp.maximum(acc.reshape(H, MB // 8, 8, C) + bias, 0.0) * mk[store][:, None]
        return z.reshape(W, C)

    def klass(r):
        return 1 if r == 0 else 2 if r == R + 1 else 0

    def strips(pairs):
        acc = jnp.dot(
            jnp.concatenate([lhs(p, (sm, s0, sp)) for p in pairs], axis=0), w1[...],
            preferred_element_type=F32,
        )
        for a, p in enumerate(pairs):
            for j in range(2):
                r = 2 * p + j
                piece = acc[a * 16 : a * 16 + 16, j * C : (j + 1) * C].reshape(2, 8, C)
                hs[r] = (jnp.maximum(piece + bias1, 0.0) * mks[klass(r)]).reshape(16, C)

    def first(pairs):
        acc = jnp.dot(
            jnp.concatenate([lhs(p, (xm, xr, xp)) for p in pairs], axis=0), w1[...],
            preferred_element_type=F32,
        )
        for a, p in enumerate(pairs):
            for j in range(2):
                r = 2 * p + j
                value = finish(acc[a * W : (a + 1) * W, j * C : (j + 1) * C], bias1, klass(r))
                side = hs[r]
                spread(value, side[0:8] * side1, side[8:16] * side0, r, h0, hm, hp)

    outs = []

    def second(pairs):
        acc = jnp.dot(
            jnp.concatenate([lhs(p, (hm, h0, hp)) for p in pairs], axis=0), w2[...],
            preferred_element_type=F32,
        )
        for a, p in enumerate(pairs):
            for j in range(2):
                ob[2 * p + j] = finish(acc[a * W : (a + 1) * W, j * C : (j + 1) * C], bias2, 0).astype(BF)

    def flush(lo, hi):
        cp = pltpu.make_async_copy(ob.at[lo:hi], out.at[lo:hi], out_sem.at[len(outs)])
        cp.start()
        outs.append(cp)

    last = R // 2
    for r in range(2, R + 2):
        image_row(r)
    strips(range(1, last))
    for p in range(1, last, 2):
        first([q for q in (p, p + 1) if q < last])
    for p in range(1, last - 1, 2):
        second([q for q in (p, p + 1) if q < last - 1])
    flush(2, R - 2)

    @pl.when(has_up)
    def _():
        r_down.wait_recv()
        r_ddn.wait_recv()
        t_down.wait_recv()
        t_ddn.wait_recv()

    @pl.when(has_down)
    def _():
        r_up.wait_recv()
        r_dup.wait_recv()
        t_up.wait_recv()
        t_dup.wait_recv()

    block_mask(2, 1)
    block_mask(3, 2)
    strip_mask(4, 1)
    strip_mask(5, 2)
    for r in (0, 1, R + 2, R + 3):
        image_row(r)
    strips((0, last))
    first((0, last))
    second((0, last - 1))
    flush(0, 2)
    flush(R - 2, R)

    r_side.wait_send()
    t_side.wait_send()

    @pl.when(has_up)
    def _():
        for cp in (r_up, r_dup, t_up, t_dup):
            cp.wait_send()

    @pl.when(has_down)
    def _():
        for cp in (r_down, r_ddn, t_down, t_ddn):
            cp.wait_send()

    for cp in outs:
        cp.wait()


def shards(image, tissue, k1, b1, k2, b2):
    R, W, C = image.shape
    H = W // MB
    any_spec = pl.BlockSpec(memory_space=pl.ANY)
    dma = pltpu.SemaphoreType.DMA
    return pl.pallas_call(
        kernel,
        out_shape=jax.ShapeDtypeStruct((R, W, C), BF),
        in_specs=[any_spec] * 6,
        out_specs=any_spec,
        scratch_shapes=[
            pltpu.VMEM((R + 4, W, C), BF),
            pltpu.VMEM((R + 4, W, C), BF),
            pltpu.VMEM((R + 4, W, C), BF),
            pltpu.VMEM((R + 4, 16, C), BF),
            pltpu.VMEM((R, 16, C), BF),
            pltpu.VMEM((R + 4, 16, C), BF),
            pltpu.VMEM((R + 4, 16, C), BF),
            pltpu.VMEM((R + 4, 16, C), BF),
            pltpu.VMEM((R + 2, W, C), BF),
            pltpu.VMEM((R + 2, W, C), BF),
            pltpu.VMEM((R + 2, W, C), BF),
            pltpu.VMEM((R + 2, 16, C), F32),
            pltpu.VMEM((12 * C, 2 * C), BF),
            pltpu.VMEM((12 * C, 2 * C), BF),
            pltpu.VMEM((2, 1, C), F32),
            pltpu.VMEM((6, 1, H), jnp.int32),
            pltpu.VMEM((3, H, 8, C), F32),
            pltpu.VMEM((3, 8, C), F32),
            pltpu.VMEM((4, W + 16, C), F32),
            pltpu.VMEM((R + 4, 32, C), F32),
            pltpu.VMEM((R, W, C), BF),
            dma((11,)),
            dma((3,)),
            dma((5,)),
            dma((5,)),
            dma((5,)),
            dma((5,)),
        ],
        compiler_params=pltpu.CompilerParams(collective_id=0, has_side_effects=True),
        name="halo_conv",
    )(
        image, tissue, k1.reshape(9 * C, C), b1.reshape(1, C), k2.reshape(9 * C, C), b2.reshape(1, C)
    )


def solution(mesh):
    in_specs = (P(("slides", "rows"), "cols", None), P(("slides", "rows"), "cols"), P(), P(), P(), P())
    return jax.shard_map(
        shards, mesh=mesh, in_specs=in_specs, out_specs=P(("slides", "rows"), "cols", None), check_vma=False
    )
```

time: 87.5 us -> 35.6 us (0.41)
  starting transfers between devices: 36 us -> 0 us
  Pallas kernels: 0 us -> 32.3 us
  other arithmetic: 18.1 us -> 0 us
  local copies, waits for them, and re-layouts: 16.6 us -> 3.14 us
  matrix products: 10.8 us -> 0 us
  waiting for transfers between devices: 5.43 us -> 0 us
    ppermute x8 -> x0, starting transfers between devices: 36 us -> none  [the longest x4 26.3 us: with_halo(): after = lax.ppermute(leading, axis, down)]
    pallas_call x0 -> x1, Pallas kernels: none -> 32.3 us  [shards(): pl.pallas_call(kernel, out_shape=jax.ShapeDtypeStruct((R, W, C), BF), in_...]
    concatenate x2 -> x0, other arithmetic: 14.7 us -> none  [conv_valid(): jnp.concatenate([padded[:, 0:cols], padded[:, 1:cols + 1], padded[:, 2:co...]
    slice x7 -> x0, local copies, waits for them, and re-layouts: 14.5 us -> none  [the longest x2 12.5 us: conv_valid(): block = wide[offset:offset + rows].reshape(rows * cols, 3 * chans)]
    dot_general x6 -> x0, matrix products: 10.8 us -> none  [conv_valid(): jnp.dot(block, kernel[offset].reshape(3 * chans, kernel.shape[3]), prefer...]
    ppermute x8 -> x0, waiting for transfers between devices: 5.43 us -> none  [the longest x4 5.42 us: with_halo(): after = lax.ppermute(leading, axis, down)]
    convert_element_type x3 -> x0, other arithmetic: 3.43 us -> none  [the longest x1 2.03 us: shards(): return (jnp.maximum(result, 0.0) * pixel_mask).astype(jnp.bfloat16)]
    unnamed x8 -> x1, local copies, waits for them, and re-layouts: 1.98 us -> 3.14 us
  transfers between devices with their start and end apart: 8 -> 0, of which waited for: 3 -> 0; matrix products, arithmetic and copies ran while one was open for 4% -> 0% of each run, Pallas kernels for 0% -> 0%
where the time goes in v1:
time: 35.6 us; the launch traced here: 35.5 us
  Pallas kernels  32.3 us (91%)
  local copies, waits for them, and re-layouts  3.14 us (9%)
    pallas_call x1, Pallas kernels, shards(): pl.pallas_call(kernel, out_shape=jax.ShapeDtypeStruct((R, W, C), BF), in_...  32.3 us
    unnamed x1, local copies, waits for them, and re-layouts  3.14 us

profile of v1, /device:TPU:37, one launch (start us, length us, event | category | flops | bytes accessed | tf_op | source)
XLA Modules:
  0.0 35.5 jit_solution(18229277934396207849)
XLA Ops:
  0.0 32.3 %halo_conv.1 = bf16[32,256,128]{2,1,0:T(8,128)(2,1)} custom-call(bf16[32,256,128]{2,1,0:T(8,128)(2,1)} %image.1, s32[1,8]{1,0:T(1,128)} %tissue.1, bf16[1152,128]{1,0:T(8,128)(2,1)} %bitcast.4, f32[1,128]{1,0:T(1,128)} %bitcast.6, bf16[1152,128]{1,0:T(8,128)(2,1)} %bitcast.5, f32[1,128]{1,0:T(1,128)} %bitcast.7), custom_call_target="tpu_custom_call" | custom-call | tf_op jit(solution)/shard_map/halo_conv/pallas_call | solution.py:274
  32.3 3.1 %copy.8 = bf16[32,256,128]{2,1,0:T(8,128)(2,1)} copy(bf16[32,256,128]{2,1,0:T(8,128)(2,1)} %halo_conv.1) | data formatting | bytes 4194304

commit v2 on v0

v2 whole, which is shorter than its diff:
```python
import jax
import jax.numpy as jnp
from jax import lax
from jax.experimental import pallas as pl
from jax.experimental.pallas import tpu as pltpu
from jax.sharding import PartitionSpec as P

MESH = pl.DeviceIdType.MESH
MB = 32
BF = jnp.bfloat16
F32 = jnp.float32
UP, DOWN, SIDE, DUP, DDN = range(5)


def spread(fb, slot, value, r, center, minus, plus):
    W = value.shape[0]
    f = fb.at[slot]
    f[8 : W + 8] = value
    minus[r] = f[7 : W + 7].astype(BF)
    plus[r] = f[9 : W + 9].astype(BF)
    if center is not None:
        center[r] = value.astype(BF)


def clear_ends(fb):
    n, L, C = fb.shape
    for k in range(n):
        fb[k, 0:8] = jnp.zeros((8, C), F32)
        fb[k, L - 8 : L] = jnp.zeros((8, C), F32)


def lhs(p, refs):
    return jnp.concatenate([ref[2 * p + k] for k in range(4) for ref in refs], axis=1)


def finish(acc, bias, mask):
    W, C = acc.shape
    z = jnp.maximum(acc.reshape(W // MB, MB // 8, 8, C) + bias, 0.0) * mask[:, None]
    return z.reshape(W, C)


def block_mask(t, mk, store):
    H, _, C = mk.shape[1:]
    for j in range(H):
        mk[store, j] = jnp.broadcast_to(t[:, j : j + 1], (8, C))


def dot(pieces, w):
    return jnp.dot(jnp.concatenate(pieces, axis=0), w[...], preferred_element_type=F32)


def interior(
    image, tissue, k1, b1, k2, b2,
    xr, xm, xp, pb, h0, hm, hp, ob, w1, w2, bs, ts, mk,
    col, fb, in_sem, send_x, recv_x, send_t, recv_t, ready,
):
    R, W, C = image.shape
    H = W // MB
    n = lax.axis_size("rows")
    sl, i, c = lax.axis_index("slides"), lax.axis_index("rows"), lax.axis_index("cols")
    has_up, has_down, first_col = i > 0, i < n - 1, c == 0
    edge = pl.multiple_of((W - 16) * (1 - c), 16)

    def load(src, dst, k):
        cp = pltpu.make_async_copy(src, dst, in_sem.at[k])
        cp.start()
        return cp

    l_top = load(image.at[0:2], xr.at[2:4], 0)
    l_bot = load(image.at[R - 2 : R], xr.at[R : R + 2], 1)
    l_col = load(image.at[:, pl.ds(edge, 16), :], col, 2)
    l_tis = load(tissue, ts.at[0], 3)
    l_w1 = [load(k1, w1.at[j * 3 * C : j * 3 * C + 9 * C, j * C : (j + 1) * C], 4 + j) for j in range(2)]
    l_img = load(image.at[2 : R - 2], xr.at[4:R], 6)
    l_b1 = load(b1, bs.at[0], 7)
    l_w2 = [load(k2, w2.at[j * 3 * C : j * 3 * C + 9 * C, j * C : (j + 1) * C], 8 + j) for j in range(2)]
    l_b2 = load(b2, bs.at[1], 10)

    up, down = (sl, i - 1, c), (sl, i + 1, c)
    dup, ddn, side = (sl, i - 1, 1 - c), (sl, i + 1, 1 - c), (sl, i, 1 - c)

    def signal(sem, dev):
        pl.semaphore_signal(sem, inc=1, device_id=dev, device_id_type=MESH)

    barrier = pltpu.get_barrier_semaphore()

    @pl.when(has_up)
    def _():
        signal(barrier, up)
        signal(barrier, dup)

    @pl.when(jnp.logical_not(first_col))
    def _():
        signal(barrier, side)

    @pl.when(jnp.logical_or(has_down, first_col))
    def _():
        pl.semaphore_wait(barrier, 2 * has_down.astype(jnp.int32) + (1 - c))

    def remote(src, dst, sends, recvs, k, dev):
        return pltpu.make_async_remote_copy(
            src_ref=src, dst_ref=dst, send_sem=sends.at[k], recv_sem=recvs.at[k],
            device_id=dev, device_id_type=MESH,
        )

    r_up = remote(xr.at[2:4], xr.at[R + 2 : R + 4], send_x, recv_x, UP, up)
    r_down = remote(xr.at[R : R + 2], xr.at[0:2], send_x, recv_x, DOWN, down)
    r_side = remote(col, pb.at[2 : R + 2], send_x, recv_x, SIDE, side)
    r_dup = remote(col.at[0:2], pb.at[R + 2 : R + 4], send_x, recv_x, DUP, dup)
    r_ddn = remote(col.at[R - 2 : R], pb.at[0:2], send_x, recv_x, DDN, ddn)
    t_side = remote(ts.at[0], ts.at[1], send_t, recv_t, SIDE, side)
    t_down = remote(ts.at[0], ts.at[2], send_t, recv_t, DOWN, down)
    t_up = remote(ts.at[0], ts.at[3], send_t, recv_t, UP, up)
    t_ddn = remote(ts.at[0], ts.at[4], send_t, recv_t, DDN, ddn)
    t_dup = remote(ts.at[0], ts.at[5], send_t, recv_t, DUP, dup)

    @pl.when(has_down)
    def _():
        signal(ready.at[0], down)
        signal(ready.at[1], ddn)

    @pl.when(first_col)
    def _():
        signal(ready.at[2], side)

    l_bot.wait()
    l_col.wait()
    l_tis.wait()

    @pl.when(has_down)
    def _():
        r_down.start()
        r_ddn.start()
        t_down.start()
        t_ddn.start()

    @pl.when(first_col)
    def _():
        r_side.start()
        t_side.start()

    for w in (w1, w2):
        w[9 * C : 12 * C, 0:C] = jnp.zeros((3 * C, C), BF)
        w[0 : 3 * C, C : 2 * C] = jnp.zeros((3 * C, C), BF)

    @pl.when(jnp.logical_not(has_up))
    def _():
        xr[0:2] = jnp.zeros((2, W, C), BF)
        pb[0:2] = jnp.zeros((2, 16, C), BF)
        ts[2] = jnp.zeros((1, H), jnp.int32)
        ts[4] = jnp.zeros((1, H), jnp.int32)

    @pl.when(jnp.logical_not(has_down))
    def _():
        xr[R + 2 : R + 4] = jnp.zeros((2, W, C), BF)
        pb[R + 2 : R + 4] = jnp.zeros((2, 16, C), BF)
        ts[3] = jnp.zeros((1, H), jnp.int32)
        ts[5] = jnp.zeros((1, H), jnp.int32)

    clear_ends(fb)
    block_mask(ts[0].astype(F32), mk, 0)
    for cp in (l_top, l_w1[0], l_w1[1], l_b1, l_b2, l_w2[0], l_w2[1], l_img):
        cp.wait()

    own = mk[0]
    counter = [0]

    def shifts(*args):
        spread(fb, counter[0] % fb.shape[0], *args)
        counter[0] += 1

    def halves(acc, pairs, bias):
        for a, p in enumerate(pairs):
            for j in range(2):
                yield 2 * p + j, finish(acc[a * W : (a + 1) * W, j * C : (j + 1) * C], bias, own)

    last = R // 2
    for r in range(2, R + 2):
        shifts(xr[r].astype(F32), r, None, xm, xp)
    for p in range(1, last, 2):
        pairs = [q for q in (p, p + 1) if q < last]
        for r, value in halves(dot([lhs(q, (xm, xr, xp)) for q in pairs], w1), pairs, bs[0]):
            shifts(value, r, h0, hm, hp)
    for p in range(1, last - 1, 2):
        pairs = [q for q in (p, p + 1) if q < last - 1]
        for r, value in halves(dot([lhs(q, (hm, h0, hp)) for q in pairs], w2), pairs, bs[1]):
            ob[r] = value.astype(BF)

    @pl.when(has_up)
    def _():
        pl.semaphore_wait(ready.at[0], 1)
        pl.semaphore_wait(ready.at[1], 1)
        r_up.start()
        r_dup.start()
        t_up.start()
        t_dup.start()

    @pl.when(jnp.logical_not(first_col))
    def _():
        pl.semaphore_wait(ready.at[2], 1)
        r_side.start()
        t_side.start()

    @pl.when(has_up)
    def _():
        for cp in (r_down, r_ddn, t_down, t_ddn):
            cp.wait_recv()
        for cp in (r_up, r_dup, t_up, t_dup):
            cp.wait_send()

    @pl.when(has_down)
    def _():
        for cp in (r_up, r_dup, t_up, t_dup):
            cp.wait_recv()
        for cp in (r_down, r_ddn, t_down, t_ddn):
            cp.wait_send()

    r_side.wait()
    t_side.wait()


def border(
    xr, xm, xp, pb, h0, hm, hp, ob, w1, w2, bs, ts, mk, out,
    ym, y0, yp, gm, g0, gp, em, e0, ep, am, ap, er, nb, mm, ms, fb, sf, hf, out_sem,
):
    R, W, C = ob.shape
    H = W // MB
    c = lax.axis_index("cols")
    left = c == 0
    near = pl.multiple_of((W - 16) * (1 - c), 16)
    far = pl.multiple_of(16 * c, 16)
    outs = []

    def flush(src, dst):
        cp = pltpu.make_async_copy(src, dst, out_sem.at[len(outs)])
        cp.start()
        outs.append(cp)

    flush(ob.at[2 : R - 2, pl.ds(far, W - 16), :], out.at[2 : R - 2, pl.ds(far, W - 16), :])

    clear_ends(fb)
    block_mask(ts[2].astype(F32), mm, 0)
    block_mask(ts[3].astype(F32), mm, 1)
    near_own = jnp.where(left, mk[0, H - 1], mk[0, 0])
    halves = []
    for own, other in ((0, 1), (2, 4), (3, 5)):
        t, o = ts[own].astype(F32), ts[other].astype(F32)
        first = jnp.where(left, t[:, H - 1 : H], o[:, H - 1 : H])
        second = jnp.where(left, o[:, 0:1], t[:, 0:1])
        k = len(halves)
        ms[k, 0] = jnp.broadcast_to(first, (8, C))
        ms[k, 1] = jnp.broadcast_to(second, (8, C))
        halves.append(k)

    bias1, bias2 = bs[0], bs[1]
    last = R // 2
    edges = (0, last)

    for k, r in enumerate((0, 1, R + 2, R + 3)):
        spread(fb, k, xr[r].astype(F32), k, None, am, ap)
    for r in range(R + 4):
        sf[r, pl.ds(pl.multiple_of(16 * c, 16), 16), :] = xr[r, pl.ds(near, 16), :].astype(F32)
        sf[r, pl.ds(pl.multiple_of(16 * (1 - c), 16), 16), :] = pb[r].astype(F32)
        ym[r] = sf[r, 7:23].astype(BF)
        y0[r] = sf[r, 8:24].astype(BF)
        yp[r] = sf[r, 9:25].astype(BF)

    def x_row(r):
        k = {0: 0, 1: 1, R + 2: 2, R + 3: 3}.get(r)
        return [xm[r], xr[r], xp[r]] if k is None else [am[k], xr[r], ap[k]]

    acc = dot(
        [lhs(p, (ym, y0, yp)) for p in range(last + 1)]
        + [jnp.concatenate([v for k in range(4) for v in x_row(2 * p + k)], axis=1) for p in edges],
        w1,
    )
    base = 16 * (last + 1)
    for a, p in enumerate(edges):
        for j in range(2):
            r = 2 * p + j
            mask = mm[0] if r == 0 else mm[1] if r == R + 1 else mk[0]
            value = finish(acc[base + a * W : base + (a + 1) * W, j * C : (j + 1) * C], bias1, mask)
            spread(fb, 2 * a + j, value, 2 * a + j, e0, em, ep)
    for p in range(last + 1):
        for j in range(2):
            r = 2 * p + j
            mask = ms[1 if r == 0 else 2 if r == R + 1 else 0]
            piece = acc[16 * p : 16 * p + 16, j * C : (j + 1) * C].reshape(2, 8, C)
            hf[r, 8:24] = (jnp.maximum(piece + bias1, 0.0) * mask).reshape(16, C)
            k = {0: 0, 1: 1, R: 2, R + 1: 3}.get(r)
            row = h0.at[r] if k is None else e0.at[k]
            rest = row[pl.ds(near, 16), :].astype(F32)
            hf[r, 0:8] = rest[0:8]
            hf[r, 24:32] = rest[8:16]
            gm[r] = hf[r, 7:23].astype(BF)
            g0[r] = hf[r, 8:24].astype(BF)
            gp[r] = hf[r, 9:25].astype(BF)

    def h_row(r):
        k = {0: 0, 1: 1, R: 2, R + 1: 3}.get(r)
        return [hm[r], h0[r], hp[r]] if k is None else [em[k], e0[k], ep[k]]

    ends = (0, last - 1)
    acc = dot(
        [jnp.concatenate([v for k in range(4) for v in h_row(2 * p + k)], axis=1) for p in ends]
        + [lhs(p, (gm, g0, gp)) for p in range(last)],
        w2,
    )
    for a, p in enumerate(ends):
        for j in range(2):
            er[2 * a + j] = finish(acc[a * W : (a + 1) * W, j * C : (j + 1) * C], bias2, mk[0]).astype(BF)
    flush(er.at[0:2, pl.ds(far, W - 16), :], out.at[0:2, pl.ds(far, W - 16), :])
    flush(er.at[2:4, pl.ds(far, W - 16), :], out.at[R - 2 : R, pl.ds(far, W - 16), :])
    for p in range(last):
        for j in range(2):
            r = 2 * p + j
            lo = 2 * W + 16 * p
            piece = acc[lo : lo + 16, j * C : (j + 1) * C].reshape(2, 8, C)
            new = jnp.maximum(jnp.where(left, piece[0], piece[1]) + bias2, 0.0) * near_own
            k = {0: 0, 1: 1, R - 2: 2, R - 1: 3}.get(r)
            row = ob.at[r] if k is None else er.at[k]
            old = row[pl.ds(near, 16), :].astype(F32)
            first = jnp.where(left, old[0:8], new)
            second = jnp.where(left, new, old[8:16])
            nb[r] = jnp.concatenate([first, second], axis=0).astype(BF)
    flush(nb, out.at[:, pl.ds(near, 16), :])
    for cp in outs:
        cp.wait()


def shards(image, tissue, k1, b1, k2, b2):
    R, W, C = image.shape
    H = W // MB
    any_spec = pl.BlockSpec(memory_space=pl.ANY)
    vmem = pl.BlockSpec(memory_space=pltpu.VMEM)
    hbm = pl.BlockSpec(memory_space=pltpu.HBM)
    dma = pltpu.SemaphoreType.DMA
    passed = [
        ((R + 4, W, C), BF), ((R + 4, W, C), BF), ((R + 4, W, C), BF), ((R + 4, 16, C), BF),
        ((R + 2, W, C), BF), ((R + 2, W, C), BF), ((R + 2, W, C), BF), ((R, W, C), BF),
        ((12 * C, 2 * C), BF), ((12 * C, 2 * C), BF), ((2, 1, C), F32), ((6, 1, H), jnp.int32),
        ((1, H, 8, C), F32),
    ]
    state = pl.pallas_call(
        interior,
        out_shape=[jax.ShapeDtypeStruct(*s) for s in passed],
        in_specs=[hbm] * 6,
        out_specs=[vmem] * len(passed),
        scratch_shapes=[
            pltpu.VMEM((R, 16, C), BF),
            pltpu.VMEM((4, W + 16, C), F32),
            dma((11,)), dma((5,)), dma((5,)), dma((5,)), dma((5,)),
            pltpu.SemaphoreType.REGULAR((3,)),
        ],
        compiler_params=pltpu.CompilerParams(
            collective_id=0, has_side_effects=True, vmem_limit_bytes=24 * 1024 * 1024
        ),
        name="interior",
    )(
        *(
            pltpu.with_memory_space_constraint(v, pltpu.HBM)
            for v in (
                image, tissue, k1.reshape(9 * C, C), b1.reshape(1, C), k2.reshape(9 * C, C), b2.reshape(1, C)
            )
        )
    )
    window = lambda rows, dtype=BF, px=16: pltpu.VMEM((rows, px, C), dtype)
    row = lambda rows: pltpu.VMEM((rows, W, C), BF)
    return pl.pallas_call(
        border,
        out_shape=jax.ShapeDtypeStruct((R, W, C), BF),
        in_specs=[vmem] * len(passed),
        out_specs=any_spec,
        scratch_shapes=[
            window(R + 4), window(R + 4), window(R + 4), window(R + 2), window(R + 2), window(R + 2),
            row(4), row(4), row(4), row(4), row(4), row(4), window(R),
            pltpu.VMEM((2, H, 8, C), F32), pltpu.VMEM((3, 2, 8, C), F32),
            pltpu.VMEM((4, W + 16, C), F32), window(R + 4, F32, 32), window(R + 2, F32, 32),
            dma((4,)),
        ],
        compiler_params=pltpu.CompilerParams(vmem_limit_bytes=24 * 1024 * 1024),
        name="border",
    )(*state)


def solution(mesh):
    in_specs = (P(("slides", "rows"), "cols", None), P(("slides", "rows"), "cols"), P(), P(), P(), P())
    return jax.shard_map(
        shards, mesh=mesh, in_specs=in_specs, out_specs=P(("slides", "rows"), "cols", None), check_vma=False
    )
```

time: 87.5 us -> 30.5 us (0.35)
  starting transfers between devices: 36 us -> 0 us
  Pallas kernels: 0 us -> 30.4 us
  other arithmetic: 18.1 us -> 0 us
  local copies, waits for them, and re-layouts: 16.6 us -> 0 us
  matrix products: 10.8 us -> 0 us
  waiting for transfers between devices: 5.43 us -> 0 us
    ppermute x8 -> x0, starting transfers between devices: 36 us -> none  [the longest x4 26.3 us: with_halo(): after = lax.ppermute(leading, axis, down)]
    pallas_call x0 -> x2, Pallas kernels: none -> 30.4 us  [the longest x1 26.2 us: shards(): pl.pallas_call(interior, out_shape=[jax.ShapeDtypeStruct(*s) for s in pas...]
    concatenate x2 -> x0, other arithmetic: 14.7 us -> none  [conv_valid(): jnp.concatenate([padded[:, 0:cols], padded[:, 1:cols + 1], padded[:, 2:co...]
    slice x7 -> x0, local copies, waits for them, and re-layouts: 14.5 us -> none  [the longest x2 12.5 us: conv_valid(): block = wide[offset:offset + rows].reshape(rows * cols, 3 * chans)]
    dot_general x6 -> x0, matrix products: 10.8 us -> none  [conv_valid(): jnp.dot(block, kernel[offset].reshape(3 * chans, kernel.shape[3]), prefer...]
    ppermute x8 -> x0, waiting for transfers between devices: 5.43 us -> none  [the longest x4 5.42 us: with_halo(): after = lax.ppermute(leading, axis, down)]
    convert_element_type x3 -> x0, other arithmetic: 3.43 us -> none  [the longest x1 2.03 us: shards(): return (jnp.maximum(result, 0.0) * pixel_mask).astype(jnp.bfloat16)]
    unnamed x8 -> x0, local copies, waits for them, and re-layouts: 1.98 us -> none
  transfers between devices with their start and end apart: 8 -> 0, of which waited for: 3 -> 0; matrix products, arithmetic and copies ran while one was open for 4% -> 0% of each run, Pallas kernels for 0% -> 0%
where the time goes in v2:
time: 30.5 us; the launch traced here: 30.4 us
  Pallas kernels  30.4 us (100%)
    pallas_call x1, Pallas kernels, shards(): pl.pallas_call(interior, out_shape=[jax.ShapeDtypeStruct(*s) for s in pas...  26.2 us
    pallas_call x1, Pallas kernels, shards(): pl.pallas_call(border, out_shape=jax.ShapeDtypeStruct((R, W, C), BF), in_...  4.13 us

profile of v2, /device:TPU:37, one launch (start us, length us, event | category | flops | bytes accessed | tf_op | source)
XLA Modules:
  0.0 30.4 jit_solution(1644599070279130803)
XLA Ops:
  0.0 26.2 %interior.1 = (bf16[36,256,128]{2,1,0:T(8,128)(2,1)S(1)}, bf16[36,256,128]{2,1,0:T(8,128)(2,1)S(1)}, bf16[36,256,128]{2,1,0:T(8,128)(2,1)S(1)}, bf16[36,16,128]{...) custom-call(bf16[32,256,128]{2,1,0:T(8,128)(2,1)} %image.1, ...), custom_call_target="tpu_custom_call" | custom-call | tf_op jit(solution)/shard_map/interior/pallas_call | solution.py:344
  26.2 4.1 %border.1 = bf16[32,256,128]{2,1,0:T(8,128)(2,1)} custom-call(bf16[36,256,128]{2,1,0:T(8,128)(2,1)S(1)} %get-tuple-element.18.xr, bf16[36,256,128]{2,1,0:T(8,128)(2,1)S(1)} %get-tuple-element.19.xm, bf16[36,256,128]{2,1,0:T(8,128)(2,1)S(1)} %get-tuple-element.20.xp, bf16[36,16,128]{2,1,0:T(8,128)(2,1)S(1)} %get-tuple-element.21.pb, ...), custom_call_target="tpu_custom_call" | custom-call | tf_op jit(solution)/shard_map/border/pallas_call | solution.py:369

commit v3 on v2

--- a/solution.py
+++ b/solution.py
@@ -12,14 +12,43 @@
 UP, DOWN, SIDE, DUP, DDN = range(5)
 
 
-def spread(fb, slot, value, r, center, minus, plus):
+def spread(fb, slot, value, r, center, minus, plus, window=None):
     W = value.shape[0]
     f = fb.at[slot]
     f[8 : W + 8] = value
+    if window is not None:
+        f[pl.ds(pl.multiple_of(W * (1 - lax.axis_index("cols")), 8), 16), :] = window
+        value = f[8 : W + 8]
     minus[r] = f[7 : W + 7].astype(BF)
     plus[r] = f[9 : W + 9].astype(BF)
     if center is not None:
         center[r] = value.astype(BF)
+
+
+def windows(xr, pb, sf, r, ym, y0, yp):
+    W = xr.shape[1]
+    c = lax.axis_index("cols")
+    near = pl.multiple_of((W - 16) * (1 - c), 16)
+    sf[r, pl.ds(pl.multiple_of(16 * c, 16), 16), :] = xr[r, pl.ds(near, 16), :].astype(F32)
+    sf[r, pl.ds(pl.multiple_of(16 * (1 - c), 16), 16), :] = pb[r].astype(F32)
+    ym[r] = sf[r, 7:23].astype(BF)
+    y0[r] = sf[r, 8:24].astype(BF)
+    yp[r] = sf[r, 9:25].astype(BF)
+
+
+def window_mask(ts, ms, k, own, other):
+    H, C = ts.shape[2], ms.shape[3]
+    left = lax.axis_index("cols") == 0
+    t, o = ts[own].astype(F32), ts[other].astype(F32)
+    first = jnp.where(left, t[:, H - 1 : H], o[:, H - 1 : H])
+    second = jnp.where(left, o[:, 0:1], t[:, 0:1])
+    ms[k, 0] = jnp.broadcast_to(first, (8, C))
+    ms[k, 1] = jnp.broadcast_to(second, (8, C))
+
+
+def window_finish(piece, bias, mask):
+    C = piece.shape[1]
+    return (jnp.maximum(piece.reshape(2, 8, C) + bias, 0.0) * mask).reshape(16, C)
 
 
 def clear_ends(fb):
@@ -29,8 +58,12 @@
         fb[k, L - 8 : L] = jnp.zeros((8, C), F32)
 
 
+def wide(pieces):
+    return jnp.concatenate(pieces, axis=1)
+
+
 def lhs(p, refs):
-    return jnp.concatenate([ref[2 * p + k] for k in range(4) for ref in refs], axis=1)
+    return wide([ref[2 * p + k] for k in range(4) for ref in refs])
 
 
 def finish(acc, bias, mask):
@@ -52,7 +85,7 @@
 def interior(
     image, tissue, k1, b1, k2, b2,
     xr, xm, xp, pb, h0, hm, hp, ob, w1, w2, bs, ts, mk,
-    col, fb, in_sem, send_x, recv_x, send_t, recv_t, ready,
+    col, fb, sf, hf, ym, y0, yp, gm, g0, gp, ms, in_sem, send_x, recv_x, send_t, recv_t, ready,
 ):
     R, W, C = image.shape
     H = W // MB
@@ -186,20 +219,88 @@
         for r, value in halves(dot([lhs(q, (hm, h0, hp)) for q in pairs], w2), pairs, bs[1]):
             ob[r] = value.astype(BF)
 
-    @pl.when(has_up)
+    @pl.when(jnp.logical_and(has_up, first_col))
+    def _():
+        pl.semaphore_wait(ready.at[1], 1)
+        r_dup.start()
+        t_dup.start()
+
+    @pl.when(jnp.logical_and(has_up, jnp.logical_not(first_col)))
     def _():
         pl.semaphore_wait(ready.at[0], 1)
-        pl.semaphore_wait(ready.at[1], 1)
         r_up.start()
-        r_dup.start()
         t_up.start()
-        t_dup.start()
 
     @pl.when(jnp.logical_not(first_col))
     def _():
         pl.semaphore_wait(ready.at[2], 1)
         r_side.start()
         t_side.start()
+
+    @pl.when(jnp.logical_and(has_up, first_col))
+    def _():
+        pl.semaphore_wait(ready.at[0], 1)
+        r_up.start()
+        t_up.start()
+
+    @pl.when(jnp.logical_and(has_up, jnp.logical_not(first_col)))
+    def _():
+        pl.semaphore_wait(ready.at[1], 1)
+        r_dup.start()
+        t_dup.start()
+
+    r_side.wait_recv()
+    t_side.wait_recv()
+
+    @pl.when(has_down)
+    def _():
+        for cp in (r_up, r_dup, t_up, t_dup):
+            cp.wait_recv()
+
+    block_mask(ts[3].astype(F32), mk, 1)
+    window_mask(ts, ms, 0, 0, 1)
+    window_mask(ts, ms, 1, 3, 5)
+    near_own = jnp.where(first_col, own[H - 1], own[0])
+    for r in range(2, R + 4):
+        windows(xr, pb, sf, r, ym, y0, yp)
+    for r in (R, R + 1, R + 2, R + 3, 2, 3):
+        shifts(xr[r].astype(F32), r, None, xm, xp, sf[r, 8:24])
+    acc = dot([lhs(p, (ym, y0, yp)) for p in range(1, last + 1)] + [lhs(last, (xm, xr, xp))], w1)
+    for p in range(1, last + 1):
+        for j in range(2):
+            r = 2 * p + j
+            piece = acc[16 * p - 16 : 16 * p, j * C : (j + 1) * C]
+            hf[r, 8:24] = window_finish(piece, bs[0], ms[1 if r == R + 1 else 0])
+            if r < R:
+                rest = h0[r, pl.ds(edge, 16), :].astype(F32)
+                hf[r, 0:8] = rest[0:8]
+                hf[r, 24:32] = rest[8:16]
+                gm[r] = hf[r, 7:23].astype(BF)
+                g0[r] = hf[r, 8:24].astype(BF)
+                gp[r] = hf[r, 9:25].astype(BF)
+    for r in (R - 2, R - 1, 2, 3):
+        shifts(h0[r].astype(F32), r, h0, hm, hp, hf[r, 8:24])
+    for j in range(2):
+        r = R + j
+        value = finish(acc[16 * last : 16 * last + W, j * C : (j + 1) * C], bs[0], mk[j])
+        shifts(value, r, h0, hm, hp, hf[r, 8:24])
+    acc = dot([lhs(p, (gm, g0, gp)) for p in range(1, last - 1)] + [lhs(last - 1, (hm, h0, hp))], w2)
+    for p in range(1, last - 1):
+        for j in range(2):
+            piece = acc[16 * p - 16 : 16 * p, j * C : (j + 1) * C].reshape(2, 8, C)
+            new = jnp.maximum(jnp.where(first_col, piece[0], piece[1]) + bs[1], 0.0) * near_own
+            ob[2 * p + j, pl.ds(pl.multiple_of((W - 8) * (1 - c), 8), 8), :] = new.astype(BF)
+    for j in range(2):
+        lo = 16 * (last - 2)
+        ob[R - 2 + j] = finish(acc[lo : lo + W, j * C : (j + 1) * C], bs[1], own).astype(BF)
+
+    r_side.wait_send()
+    t_side.wait_send()
+
+    @pl.when(has_down)
+    def _():
+        for cp in (r_down, r_ddn, t_down, t_ddn):
+            cp.wait_send()
 
     @pl.when(has_up)
     def _():
@@ -208,124 +309,36 @@
         for cp in (r_up, r_dup, t_up, t_dup):
             cp.wait_send()
 
-    @pl.when(has_down)
-    def _():
-        for cp in (r_up, r_dup, t_up, t_dup):
-            cp.wait_recv()
-        for cp in (r_down, r_ddn, t_down, t_ddn):
-            cp.wait_send()
-
-    r_side.wait()
-    t_side.wait()
-
-
-def border(
+
+def top(
     xr, xm, xp, pb, h0, hm, hp, ob, w1, w2, bs, ts, mk, out,
-    ym, y0, yp, gm, g0, gp, em, e0, ep, am, ap, er, nb, mm, ms, fb, sf, hf, out_sem,
+    ym, y0, yp, am, ap, em, e0, ep, er, mm, ms, fb, sf, out_sem,
 ):
     R, W, C = ob.shape
-    H = W // MB
-    c = lax.axis_index("cols")
-    left = c == 0
-    near = pl.multiple_of((W - 16) * (1 - c), 16)
-    far = pl.multiple_of(16 * c, 16)
-    outs = []
-
-    def flush(src, dst):
-        cp = pltpu.make_async_copy(src, dst, out_sem.at[len(outs)])
-        cp.start()
-        outs.append(cp)
-
-    flush(ob.at[2 : R - 2, pl.ds(far, W - 16), :], out.at[2 : R - 2, pl.ds(far, W - 16), :])
-
+    rest = pltpu.make_async_copy(ob.at[2:R], out.at[2:R], out_sem.at[0])
+    rest.start()
     clear_ends(fb)
     block_mask(ts[2].astype(F32), mm, 0)
-    block_mask(ts[3].astype(F32), mm, 1)
-    near_own = jnp.where(left, mk[0, H - 1], mk[0, 0])
-    halves = []
-    for own, other in ((0, 1), (2, 4), (3, 5)):
-        t, o = ts[own].astype(F32), ts[other].astype(F32)
-        first = jnp.where(left, t[:, H - 1 : H], o[:, H - 1 : H])
-        second = jnp.where(left, o[:, 0:1], t[:, 0:1])
-        k = len(halves)
-        ms[k, 0] = jnp.broadcast_to(first, (8, C))
-        ms[k, 1] = jnp.broadcast_to(second, (8, C))
-        halves.append(k)
-
-    bias1, bias2 = bs[0], bs[1]
-    last = R // 2
-    edges = (0, last)
-
-    for k, r in enumerate((0, 1, R + 2, R + 3)):
-        spread(fb, k, xr[r].astype(F32), k, None, am, ap)
-    for r in range(R + 4):
-        sf[r, pl.ds(pl.multiple_of(16 * c, 16), 16), :] = xr[r, pl.ds(near, 16), :].astype(F32)
-        sf[r, pl.ds(pl.multiple_of(16 * (1 - c), 16), 16), :] = pb[r].astype(F32)
-        ym[r] = sf[r, 7:23].astype(BF)
-        y0[r] = sf[r, 8:24].astype(BF)
-        yp[r] = sf[r, 9:25].astype(BF)
-
-    def x_row(r):
-        k = {0: 0, 1: 1, R + 2: 2, R + 3: 3}.get(r)
-        return [xm[r], xr[r], xp[r]] if k is None else [am[k], xr[r], ap[k]]
-
-    acc = dot(
-        [lhs(p, (ym, y0, yp)) for p in range(last + 1)]
-        + [jnp.concatenate([v for k in range(4) for v in x_row(2 * p + k)], axis=1) for p in edges],
-        w1,
-    )
-    base = 16 * (last + 1)
-    for a, p in enumerate(edges):
-        for j in range(2):
-            r = 2 * p + j
-            mask = mm[0] if r == 0 else mm[1] if r == R + 1 else mk[0]
-            value = finish(acc[base + a * W : base + (a + 1) * W, j * C : (j + 1) * C], bias1, mask)
-            spread(fb, 2 * a + j, value, 2 * a + j, e0, em, ep)
-    for p in range(last + 1):
-        for j in range(2):
-            r = 2 * p + j
-            mask = ms[1 if r == 0 else 2 if r == R + 1 else 0]
-            piece = acc[16 * p : 16 * p + 16, j * C : (j + 1) * C].reshape(2, 8, C)
-            hf[r, 8:24] = (jnp.maximum(piece + bias1, 0.0) * mask).reshape(16, C)
-            k = {0: 0, 1: 1, R: 2, R + 1: 3}.get(r)
-            row = h0.at[r] if k is None else e0.at[k]
-            rest = row[pl.ds(near, 16), :].astype(F32)
-            hf[r, 0:8] = rest[0:8]
-            hf[r, 24:32] = rest[8:16]
-            gm[r] = hf[r, 7:23].astype(BF)
-            g0[r] = hf[r, 8:24].astype(BF)
-            gp[r] = hf[r, 9:25].astype(BF)
-
-    def h_row(r):
-        k = {0: 0, 1: 1, R: 2, R + 1: 3}.get(r)
-        return [hm[r], h0[r], hp[r]] if k is None else [em[k], e0[k], ep[k]]
-
-    ends = (0, last - 1)
-    acc = dot(
-        [jnp.concatenate([v for k in range(4) for v in h_row(2 * p + k)], axis=1) for p in ends]
-        + [lhs(p, (gm, g0, gp)) for p in range(last)],
-        w2,
-    )
-    for a, p in enumerate(ends):
-        for j in range(2):
-            er[2 * a + j] = finish(acc[a * W : (a + 1) * W, j * C : (j + 1) * C], bias2, mk[0]).astype(BF)
-    flush(er.at[0:2, pl.ds(far, W - 16), :], out.at[0:2, pl.ds(far, W - 16), :])
-    flush(er.at[2:4, pl.ds(far, W - 16), :], out.at[R - 2 : R, pl.ds(far, W - 16), :])
-    for p in range(last):
-        for j in range(2):
-            r = 2 * p + j
-            lo = 2 * W + 16 * p
-            piece = acc[lo : lo + 16, j * C : (j + 1) * C].reshape(2, 8, C)
-            new = jnp.maximum(jnp.where(left, piece[0], piece[1]) + bias2, 0.0) * near_own
-            k = {0: 0, 1: 1, R - 2: 2, R - 1: 3}.get(r)
-            row = ob.at[r] if k is None else er.at[k]
-            old = row[pl.ds(near, 16), :].astype(F32)
-            first = jnp.where(left, old[0:8], new)
-            second = jnp.where(left, new, old[8:16])
-            nb[r] = jnp.concatenate([first, second], axis=0).astype(BF)
-    flush(nb, out.at[:, pl.ds(near, 16), :])
-    for cp in outs:
-        cp.wait()
+    window_mask(ts, ms, 0, 2, 4)
+    window_mask(ts, ms, 1, 0, 1)
+    for r in range(4):
+        windows(xr, pb, sf, r, ym, y0, yp)
+    for r in range(2):
+        spread(fb, r, xr[r].astype(F32), r, None, am, ap, sf[r, 8:24])
+    rows = [(am, xr, ap), (am, xr, ap), (xm, xr, xp), (xm, xr, xp)]
+    acc = dot([lhs(0, (ym, y0, yp)), wide([ref[k] for k in range(4) for ref in rows[k]])], w1)
+    for j in range(2):
+        part = acc[:, j * C : (j + 1) * C]
+        window = window_finish(part[0:16], bs[0], ms[j])
+        spread(fb, 2 + j, finish(part[16 : 16 + W], bs[0], mk[0] if j else mm[0]), j, e0, em, ep, window)
+    rows = [(em, e0, ep), (em, e0, ep), (hm, h0, hp), (hm, h0, hp)]
+    acc = dot([wide([ref[k] for k in range(4) for ref in rows[k]])], w2)
+    for j in range(2):
+        er[j] = finish(acc[:, j * C : (j + 1) * C], bs[1], mk[0]).astype(BF)
+    first = pltpu.make_async_copy(er, out.at[0:2], out_sem.at[1])
+    first.start()
+    rest.wait()
+    first.wait()
 
 
 def shards(image, tissue, k1, b1, k2, b2):
@@ -339,16 +352,20 @@
         ((R + 4, W, C), BF), ((R + 4, W, C), BF), ((R + 4, W, C), BF), ((R + 4, 16, C), BF),
         ((R + 2, W, C), BF), ((R + 2, W, C), BF), ((R + 2, W, C), BF), ((R, W, C), BF),
         ((12 * C, 2 * C), BF), ((12 * C, 2 * C), BF), ((2, 1, C), F32), ((6, 1, H), jnp.int32),
-        ((1, H, 8, C), F32),
+        ((2, H, 8, C), F32),
     ]
+    window = lambda rows, dtype=BF, px=16: pltpu.VMEM((rows, px, C), dtype)
+    row = lambda rows: pltpu.VMEM((rows, W, C), BF)
     state = pl.pallas_call(
         interior,
         out_shape=[jax.ShapeDtypeStruct(*s) for s in passed],
         in_specs=[hbm] * 6,
         out_specs=[vmem] * len(passed),
         scratch_shapes=[
-            pltpu.VMEM((R, 16, C), BF),
-            pltpu.VMEM((4, W + 16, C), F32),
+            window(R),
+            pltpu.VMEM((4, W + 16, C), F32), window(R + 4, F32, 32), window(R + 2, F32, 32),
+            window(R + 4), window(R + 4), window(R + 4), window(R + 2), window(R + 2), window(R + 2),
+            pltpu.VMEM((2, 2, 8, C), F32),
             dma((11,)), dma((5,)), dma((5,)), dma((5,)), dma((5,)),
             pltpu.SemaphoreType.REGULAR((3,)),
         ],
@@ -364,19 +381,17 @@
             )
         )
     )
-    window = lambda rows, dtype=BF, px=16: pltpu.VMEM((rows, px, C), dtype)
-    row = lambda rows: pltpu.VMEM((rows, W, C), BF)
     return pl.pallas_call(
-        border,
+        top,
         out_shape=jax.ShapeDtypeStruct((R, W, C), BF),
         in_specs=[vmem] * len(passed),
         out_specs=any_spec,
         scratch_shapes=[
-            window(R + 4), window(R + 4), window(R + 4), window(R + 2), window(R + 2), window(R + 2),
-            row(4), row(4), row(4), row(4), row(4), row(4), window(R),
-            pltpu.VMEM((2, H, 8, C), F32), pltpu.VMEM((3, 2, 8, C), F32),
-            pltpu.VMEM((4, W + 16, C), F32), window(R + 4, F32, 32), window(R + 2, F32, 32),
-            dma((4,)),
+            window(4), window(4), window(4),
+            row(2), row(2), row(2), row(2), row(2), row(2),
+            pltpu.VMEM((1, H, 8, C), F32), pltpu.VMEM((2, 2, 8, C), F32),
+            pltpu.VMEM((4, W + 16, C), F32), window(4, F32, 32),
+            dma((2,)),
         ],
         compiler_params=pltpu.CompilerParams(vmem_limit_bytes=24 * 1024 * 1024),
         name="border",

time: 30.5 us -> 26.7 us (0.88)
  Pallas kernels: 30.4 us -> 26.6 us
    pallas_call x1, Pallas kernels: 4.13 us -> 1.95 us  [shards(): pl.pallas_call(top, out_shape=jax.ShapeDtypeStruct((R, W, C), BF), in_spe...]
    pallas_call x1, Pallas kernels: 26.2 us -> 24.6 us  [shards(): pl.pallas_call(interior, out_shape=[jax.ShapeDtypeStruct(*s) for s in pas...]
where the time goes in v3:
time: 26.7 us; the launch traced here: 26.6 us
  Pallas kernels  26.6 us (100%)
    pallas_call x1, Pallas kernels, shards(): pl.pallas_call(interior, out_shape=[jax.ShapeDtypeStruct(*s) for s in pas...  24.6 us
    pallas_call x1, Pallas kernels, shards(): pl.pallas_call(top, out_shape=jax.ShapeDtypeStruct((R, W, C), BF), in_spe...  1.95 us

profile of v3, /device:TPU:37, one launch (start us, length us, event | category | flops | bytes accessed | tf_op | source)
XLA Modules:
  0.0 26.6 jit_solution(5585472085661288799)
XLA Ops:
  0.0 24.6 %interior.1 = (bf16[36,256,128]{2,1,0:T(8,128)(2,1)S(1)}, bf16[36,256,128]{2,1,0:T(8,128)(2,1)S(1)}, bf16[36,256,128]{2,1,0:T(8,128)(2,1)S(1)}, bf16[36,16,128]{...) custom-call(bf16[32,256,128]{2,1,0:T(8,128)(2,1)} %image.1, ...), custom_call_target="tpu_custom_call" | custom-call | tf_op jit(solution)/shard_map/interior/pallas_call | solution.py:359
  24.6 2.0 %border.1 = bf16[32,256,128]{2,1,0:T(8,128)(2,1)} custom-call(bf16[36,256,128]{2,1,0:T(8,128)(2,1)S(1)} %get-tuple-element.18.xr, bf16[36,256,128]{2,1,0:T(8,128)(2,1)S(1)} %get-tuple-element.19.xm, bf16[36,256,128]{2,1,0:T(8,128)(2,1)S(1)} %get-tuple-element.20.xp, bf16[36,16,128]{2,1,0:T(8,128)(2,1)S(1)} %get-tuple-element.21.pb, ...), custom_call_target="tpu_custom_call" | custom-call | tf_op jit(solution)/shard_map/border/pallas_call | solution.py:384
